TPU v7x, 32 devices: a whole 2x2x4 slice. The times are simulated.
32 devices in a mesh: shard: 8 (over z, x), tp: 4 (over y, core).
Axes of the slice: x: 2, y: 2, z: 4, core: 2. Of those that a mesh axis runs over, the one named last changes fastest.
Arguments:
- one_gate: float32 [2048, 8192], P('shard', 'tp'), may hold values from -0.1875 to 0.1875
- other_gate: float32 [2048, 8192], P('shard', 'tp'), may hold values from -0.125 to 0.125
- one_up: float32 [2048, 8192], P('shard', 'tp'), may hold values from -0.1875 to 0.1875
- other_up: float32 [2048, 8192], P('shard', 'tp'), may hold values from -0.125 to 0.125
- mix_share: float32 [2048], P('shard'), may hold values from 0.2 to 0.8
- norm_train: float32 [2048], P(('shard', 'tp')), may hold values from 0.25 to 1.75
- norm_step: float32 [2048], P(('shard', 'tp')), may hold values from -0.3 to 0.3
Outputs:
- serve_gate: bfloat16 [2048, 8192], P(None, 'tp')
- serve_up: bfloat16 [2048, 8192], P(None, 'tp')
- factor_gate: float32 [8192], P('tp')
- factor_up: float32 [8192], P('tp')
- serve_norm: bfloat16 [2048], replicated
All inputs are finite; a program needn't handle non-finite values.
Results may differ from a plain program's by a relative error of at most 0.0004.
Values may be sent and summed in bfloat16 or wider, within the bound.
A program may use at most 128 MiB of HBM per device.

v0:
```python
import jax
import jax.numpy as jnp
from jax import lax
from jax.sharding import PartitionSpec as P


def shards(one_gate, other_gate, one_up, other_up, mix_share, norm_train, norm_step):
    fresh_gate = mix_share[:, None] * one_gate + (1.0 - mix_share[:, None]) * other_gate
    fresh_up = mix_share[:, None] * one_up + (1.0 - mix_share[:, None]) * other_up
    total_gate, total_up = lax.psum(
        (jnp.sum(fresh_gate * fresh_gate, axis=0), jnp.sum(fresh_up * fresh_up, axis=0)), "shard"
    )
    factor_gate = jnp.sqrt(total_gate)
    factor_up = jnp.sqrt(total_up)
    narrow_gate, narrow_up = (
        (fresh_gate / factor_gate).astype(jnp.bfloat16),
        (fresh_up / factor_up).astype(jnp.bfloat16),
    )
    serve_gate, serve_up = (
        lax.all_gather(narrow_gate, "shard", axis=0, tiled=True),
        lax.all_gather(narrow_up, "shard", axis=0, tiled=True),
    )
    serve_norm = lax.all_gather(
        (norm_train + norm_step).astype(jnp.bfloat16), ("shard", "tp"), axis=0, tiled=True
    )
    return (serve_gate, serve_up, factor_gate, factor_up, serve_norm)


def solution(mesh):
    return jax.shard_map(
        shards,
        mesh=mesh,
        in_specs=(
            P("shard", "tp"),
            P("shard", "tp"),
            P("shard", "tp"),
            P("shard", "tp"),
            P("shard"),
            P(("shard", "tp")),
            P(("shard", "tp")),
        ),
        out_specs=(P(None, "tp"), P(None, "tp"), P("tp"), P("tp"), P()),
        check_vma=False,
    )
```

profile of v0, /device:TPU:0, one launch (start us, length us, event | category | flops | bytes accessed | tf_op | source)
XLA Modules:
  0.0 329.1 jit_solution(13324231435357254434)
XLA Ops:
  7.2 0.0 all-gather.3.cloned.1.call-start
  7.2 0.7 broadcast_subtract_fusion
  7.9 0.0 copy-start
  7.9 0.0 copy-start.3
  7.9 4.8 %multiply_reduce_fusion = (f32[2048]{0:T(1024)S(1)}, f32[2048]{0:T(1024)S(1)}) fusion(f32[256,2048]{1,0:T(8,128)} %param.10, f32[256]{0:T(256)S(1)} %broadcast_subtract_fusion, f32[256,2048]{1,0:T(8,128)} %param.9, f32[256]{0:T(256)} %param.11, f32[256,2048]{1,0:T(8,128)} %param.8, f32[256,2048]{1,0:T(8,128)} %param.7), kind=kLoop, calls=%fused_computation.1 | loop fusion | flops 5238784 | bytes 8407040 | tf_op jit(solution)/shard_map/reduce_sum | solution.py:11
  12.7 38.8 %all-reduce.1 = (f32[2048]{0:T(1024)S(1)}, f32[2048]{0:T(1024)S(1)}) all-reduce(f32[2048]{0:T(1024)S(1)} %get-tuple-element.6, f32[2048]{0:T(1024)S(1)} %get-tuple-element.5), channel_id=1, replica_groups=mesh['shard'=8,'tp'=4] {'shard'}, use_global_device_ids=true, to_apply=%region_1.0 | all-reduce | flops 4096 | bytes 32768 | tf_op jit(solution)/shard_map/psum | solution.py:10
  51.5 0.0 copy-start.1
  51.5 0.0 copy-done
  51.5 0.0 copy-done.3
  51.6 0.0 copy-start.2
  51.6 5.4 %divide_convert_fusion = (bf16[256,2048]{1,0:T(8,128)(2,1)}, bf16[256,2048]{1,0:T(8,128)(2,1)}) fusion(f32[2048]{0:T(1024)S(1)} %sqrt.7, f32[256,2048]{1,0:T(8,128)S(1)} %copy-done, f32[256]{0:T(256)S(1)} %broadcast_subtract_fusion, f32[256,2048]{1,0:T(8,128)} %param.9, f32[256]{0:T(256)S(1)} %copy-done.3, f32[2048]{0:T(1024)S(1)} %sqrt.6, ...), kind=kLoop, calls=%fused_computation | loop fusion | flops 5242880 | bytes 10504192 | tf_op jit(solution)/shard_map/convert_element_type | solution.py:17
  56.9 0.0 copy-done.1
  56.9 0.0 copy-done.2
  56.9 0.0 copy-start.4
  56.9 0.0 copy-start.5
  56.9 0.0 all-gather.3.cloned.1.call-update
  57.0 0.0 all-gather.5.cloned.1.call-start
  57.0 0.7 all-gather.5.cloned.1.call-update
  57.7 0.0 copy-done.4
  57.7 0.0 copy-done.5
  57.8 0.2 dynamic-update-slice
  58.0 41.0 %all-reduce = bf16[2048]{0:T(1024)(128)(2,1)} all-reduce(bf16[2048]{0:T(1024)(128)(2,1)S(1)} %dynamic-update-slice), channel_id=1, replica_groups=mesh['shard'=8,'tp'=4] {'shard','tp'}, use_global_device_ids=true, to_apply=%add | all-reduce | flops 2048 | bytes 8192
  99.0 81.0 %all-gather.3.cloned.1.call-done = bf16[2048,2048]{1,0:T(8,128)(2,1)} async-done(((bf16[256,2048]{1,0:T(8,128)(2,1)}), bf16[2048,2048]{1,0:T(8,128)(2,1)}) %all-gather.3.cloned.1.call-update) | async-done | bytes 8388624 | tf_op jit(solution)/shard_map/all_gather | solution.py:20
  180.0 125.4 %all-gather.5.cloned.1.call-done = bf16[2048,2048]{1,0:T(8,128)(2,1)} async-done(((bf16[256,2048]{1,0:T(8,128)(2,1)}), bf16[2048,2048]{1,0:T(8,128)(2,1)}) %all-gather.5.cloned.1.call-update) | async-done | bytes 8388624 | tf_op jit(solution)/shard_map/all_gather | solution.py:21
  305.3 8.4 %copy.15 = bf16[2048,2048]{1,0:T(8,128)(2,1)} copy(bf16[2048,2048]{1,0:T(8,128)(2,1)} %all-gather.3.cloned.1.call-done) | data formatting | bytes 16777216
  313.8 8.4 %copy.16 = bf16[2048,2048]{1,0:T(8,128)(2,1)} copy(bf16[2048,2048]{1,0:T(8,128)(2,1)} %all-gather.5.cloned.1.call-done) | data formatting | bytes 16777216
  (4 shorter events, 0.0 us)
Async XLA Ops:
  7.2 172.8 %all-gather.3.cloned.1.call-start = ((), (), s32[]{:S(2)}) async-start(), calls=%async_computation | async-start | bytes 9437184 | tf_op jit(solution)/shard_map/all_gather | solution.py:20
  7.9 43.6 %copy-start = (f32[256,2048]{1,0:T(8,128)S(1)}, f32[256,2048]{1,0:T(8,128)}, u32[]{:S(2)}) copy-start(f32[256,2048]{1,0:T(8,128)} %param.10) | copy-start | bytes 6291460
  7.9 43.7 %copy-start.3 = (f32[256]{0:T(256)S(1)}, f32[256]{0:T(256)}, u32[]{:S(2)}) copy-start(f32[256]{0:T(256)} %param.11) | copy-start | bytes 3076
  51.5 5.4 %copy-start.1 = (f32[2048]{0:T(1024)}, f32[2048]{0:T(1024)S(1)}, u32[]{:S(2)}) copy-start(f32[2048]{0:T(1024)S(1)} %sqrt.6) | copy-start | bytes 24580
  51.6 5.4 %copy-start.2 = (f32[2048]{0:T(1024)}, f32[2048]{0:T(1024)S(1)}, u32[]{:S(2)}) copy-start(f32[2048]{0:T(1024)S(1)} %sqrt.7) | copy-start | bytes 24580
  56.9 0.8 copy-start.4
  56.9 0.8 copy-start.5
  57.0 248.4 %all-gather.5.cloned.1.call-start = ((), (), s32[]{:S(2)}) async-start(), calls=%async_computation.1 | async-start | bytes 9437184 | tf_op jit(solution)/shard_map/all_gather | solution.py:21
Sparse Core Ops, SparseCore 0:
  57.1 122.8 all-gather.2
  182.7 122.6 all-gather.4
where the time goes:
time: 329 us
  waiting for transfers between devices  207 us (63%)
  blocking collectives  79.8 us (24%)
  local copies, waits for them, and re-layouts  17.2 us (5%)
  between operations  14.1 us (4%)
  other arithmetic  10.8 us (3%)
    all_gather x1, waiting for transfers between devices, shards(): lax.all_gather(narrow_up, 'shard', axis=0, tiled=True)  125 us
    all_gather x1, waiting for transfers between devices, shards(): lax.all_gather(narrow_gate, 'shard', axis=0, tiled=True)  81 us
    unnamed x1, blocking collectives  41 us
    psum x1, blocking collectives, shards(): lax.psum((jnp.sum(fresh_gate * fresh_gate, axis=0), jnp.sum(fresh_up * fr...  38.8 us
    unnamed x16, local copies, waits for them, and re-layouts  17.2 us
  transfers between devices with their start and end apart: 2, of which 2 were waited for; matrix products, arithmetic and copies ran while one was open for 0% of the time, Pallas kernels for 0%

commit v1 on v0

v1 whole, which is shorter than its diff:
```python
import functools

import jax
import jax.numpy as jnp
from jax import lax
from jax.experimental import pallas as pl
from jax.experimental.pallas import tpu as pltpu
from jax.sharding import PartitionSpec as P

MESH = pl.DeviceIdType.MESH
UP, DOWN, ACROSS = 0, 1, 2


def gather_kernel(
    n, parts, pieces, one_gate, other_gate, one_up, other_up, mix, train, step,
    held, factor, norm,
    ones, others, sums, in_sem, sum_send, sum_recv, norm_send, norm_recv, send_sem, recv_sem,
):
    me = lax.axis_index("shard")
    part = lax.axis_index("tp")
    m, half = n // 2, pieces // 2
    place, side = me // 2, me % 2
    rows, cols = ones.shape[1:]
    tall = rows // half

    def reads(piece):
        a, at = piece // half, pl.ds(piece % half * tall, tall)
        first, second = ((one_gate, other_gate), (one_up, other_up))[a]
        return (
            pltpu.make_async_copy(first.at[at], ones.at[a, at], in_sem.at[0, piece]),
            pltpu.make_async_copy(second.at[at], others.at[a, at], in_sem.at[1, piece]),
        )

    for piece in range(pieces):
        for copy in reads(piece):
            copy.start()

    barrier = pltpu.get_barrier_semaphore()

    @pl.loop(1, n)
    def _(off):
        pl.semaphore_signal(barrier, inc=1, device_id={"shard": lax.rem(me + off, n)}, device_id_type=MESH)

    @pl.loop(1, parts)
    def _(off):
        pl.semaphore_signal(barrier, inc=1, device_id={"tp": lax.rem(part + off, parts)}, device_id_type=MESH)

    pl.semaphore_wait(barrier, n + parts - 2)

    norm[me, part] = train[...] + step[...]

    def norm_row(off):
        return pltpu.make_async_remote_copy(
            src_ref=norm.at[me, part], dst_ref=norm.at[me, part],
            send_sem=norm_send.at[off], recv_sem=norm_recv.at[off],
            device_id={"tp": lax.rem(part + off, parts)}, device_id_type=MESH,
        )

    def norm_group(off):
        return pltpu.make_async_remote_copy(
            src_ref=norm.at[me], dst_ref=norm.at[me],
            send_sem=norm_send.at[parts + off], recv_sem=norm_recv.at[parts + off],
            device_id={"shard": lax.rem(me + off, n)}, device_id_type=MESH,
        )

    @pl.loop(1, parts)
    def _(off):
        norm_row(off).start()

    for a in range(2):
        total = jnp.zeros((8, cols), jnp.float32)
        for piece in range(a * half, (a + 1) * half):
            for copy in reads(piece):
                copy.wait()

            def mixed(r, total):
                at = pl.ds(pl.multiple_of(piece % half * tall + r * 8, 8), 8)
                share = mix[at]
                fresh = share * ones[a, at] + (1.0 - share) * others[a, at]
                ones[a, at] = fresh
                return total + fresh * fresh

            total = lax.fori_loop(0, tall // 8, mixed, total)
        sums[me, pl.ds(a, 1)] = jnp.sum(total, axis=0, keepdims=True)

    def sum_copy(off):
        return pltpu.make_async_remote_copy(
            src_ref=sums.at[me], dst_ref=sums.at[me],
            send_sem=sum_send.at[off], recv_sem=sum_recv.at[off],
            device_id={"shard": lax.rem(me + off, n)}, device_id_type=MESH,
        )

    @pl.loop(1, n)
    def _(off):
        sum_copy(off).start()

    @pl.loop(1, parts)
    def _(off):
        norm_row(off).wait()

    @pl.loop(1, n)
    def _(off):
        norm_group(off).start()

    @pl.loop(1, n)
    def _(off):
        sum_copy(off).wait_recv()

    factors = jnp.sqrt(lax.fori_loop(1, n, lambda i, t: t + sums[i], sums[0]))
    factor[...] = factors
    scales = 1.0 / factors

    def piece_of(j, s, c):
        at = pl.multiple_of((2 * j + s) * rows + c % half * tall, 8)
        return held.at[c // half, pl.ds(at, tall)]

    def send(way, j, s, c, slot=None):
        target = {
            UP: {"shard": lax.rem(me + 2, n)},
            DOWN: {"shard": lax.rem(me + n - 2, n)},
            ACROSS: {"shard": 2 * place + 1 - side},
        }[way]
        block = piece_of(j, s, c)
        return pltpu.make_async_remote_copy(
            src_ref=block, dst_ref=block,
            send_sem=send_sem.at[way * m + j if slot is None else slot, c],
            recv_sem=recv_sem.at[2 * j + s, c],
            device_id=target, device_id_type=MESH,
        )

    def arrived(j, s, c):
        block = piece_of(j, s, c)
        pltpu.make_async_copy(block, block, recv_sem.at[2 * j + s, c]).wait()

    last = m - 1
    first_place, last_place = place == 0, place == last

    def crosses(j, c):
        kept = (first_place & (j == 1)) | (last_place & (j == last - 1))
        kept = kept & (c >= half)
        return ~(kept | ((place == 1) & (j == 0)) | ((place == last - 1) & (j == last)))

    for c in range(pieces):
        a, at = c // half, c % half * tall
        scale = scales[a : a + 1]

        def scaled(r, _):
            here = pl.multiple_of(at + r * 8, 8)
            there = pl.multiple_of(me * rows + at + r * 8, 8)
            held[a, pl.ds(there, 8)] = (ones[a, pl.ds(here, 8)] * scale).astype(jnp.bfloat16)
            return 0

        lax.fori_loop(0, tall // 8, scaled, 0)

        @pl.when(~last_place)
        def _():
            send(UP, place, side, c).start()

        @pl.when(~first_place)
        def _():
            send(DOWN, place, side, c).start()

        send(ACROSS, place, side, c).start()

    extra = 3 * m

    def ends(b, c):
        return (first_place | last_place) & (b == 1)

    def inner(b, c):
        return ((place == 1) | (place == last - 1)) & (b == last - 1) & (c >= half)

    @pl.loop(0, last * pieces)
    def _(slot):
        b, c = slot // pieces, slot % pieces

        @pl.when(b < place)
        def _():
            j = place - 1 - b
            arrived(j, side, c)

            @pl.when(~last_place)
            def _():
                send(UP, j, side, c).start()

            @pl.when(crosses(j, c))
            def _():
                send(ACROSS, j, side, c).start()

        @pl.when(b < last - place)
        def _():
            j = place + 1 + b
            arrived(j, side, c)

            @pl.when(~first_place)
            def _():
                send(DOWN, j, side, c).start()

            @pl.when(crosses(j, c))
            def _():
                send(ACROSS, j, side, c).start()

        @pl.when(ends(b, c) | inner(b, c))
        def _():
            arrived(place, 1 - side, c)

            @pl.when(first_place | (place == last - 1))
            def _():
                send(UP, place, 1 - side, c, extra).start()

            @pl.when(last_place | (place == 1))
            def _():
                send(DOWN, place, 1 - side, c, extra).start()

    @pl.loop(0, m * pieces)
    def _(slot):
        j, c = slot // pieces, slot % pieces
        passed_on = first_place | last_place | (((place == 1) | (place == last - 1)) & (c >= half))

        @pl.when(~((j == place) & passed_on))
        def _():
            arrived(j, 1 - side, c)

        @pl.when((j <= place) & ~last_place)
        def _():
            send(UP, j, side, c).wait_send()

        @pl.when((j >= place) & ~first_place)
        def _():
            send(DOWN, j, side, c).wait_send()

        @pl.when(crosses(j, c))
        def _():
            send(ACROSS, j, side, c).wait_send()

        @pl.when((j == place) & passed_on)
        def _():
            send(UP, place, 1 - side, c, extra).wait_send()

    @pl.loop(1, n)
    def _(off):
        sum_copy(off).wait_send()
        norm_group(off).wait()


def write_kernel(n, held, gate, up, sem):
    rows = held.shape[1] // n
    copies = [
        pltpu.make_async_copy(held.at[a, pl.ds(i * rows, rows)], out.at[pl.ds(i * rows, rows)], sem.at[a, i])
        for i in range(n)
        for a, out in enumerate((gate, up))
    ]
    for copy in copies:
        copy.start()
    for copy in copies:
        copy.wait()


def shards(n, parts, one_gate, other_gate, one_up, other_up, mix_share, norm_train, norm_step):
    rows, cols = one_gate.shape
    few = norm_train.shape[0]
    pieces = 2 * max(1, rows // 64)
    kinds = pltpu.SemaphoreType
    vmem, anywhere = pl.BlockSpec(memory_space=pltpu.VMEM), pl.BlockSpec(memory_space=pl.ANY)
    held, factors, norm = pl.pallas_call(
        functools.partial(gather_kernel, n, parts, pieces),
        out_shape=(
            pltpu.VMEM((2, n * rows, cols), jnp.bfloat16),
            jax.ShapeDtypeStruct((2, cols), jnp.float32),
            jax.ShapeDtypeStruct((n, parts, 1, few), jnp.float32),
        ),
        in_specs=[anywhere] * 4 + [vmem] * 3,
        out_specs=(vmem, vmem, vmem),
        scratch_shapes=[
            pltpu.VMEM((2, rows, cols), jnp.float32),
            pltpu.VMEM((2, rows, cols), jnp.float32),
            pltpu.VMEM((n, 2, cols), jnp.float32),
            kinds.DMA((2, pieces)),
            kinds.DMA((n,)),
            kinds.DMA((n,)),
            kinds.DMA((n + parts,)),
            kinds.DMA((n + parts,)),
            kinds.DMA((3 * (n // 2) + 1, pieces)),
            kinds.DMA((n, pieces)),
        ],
        compiler_params=pltpu.CompilerParams(
            collective_id=0, has_side_effects=True, vmem_limit_bytes=36 * 2**20
        ),
        name="mix_gather",
    )(
        one_gate, other_gate, one_up, other_up, mix_share[:, None],
        norm_train[None], norm_step[None],
    )
    gate, up = pl.pallas_call(
        functools.partial(write_kernel, n),
        out_shape=(jax.ShapeDtypeStruct((n * rows, cols), jnp.bfloat16),) * 2,
        in_specs=[vmem],
        out_specs=(anywhere, anywhere),
        scratch_shapes=[kinds.DMA((2, n))],
        compiler_params=pltpu.CompilerParams(vmem_limit_bytes=20 * 2**20),
        name="write_out",
    )(held)
    return gate, up, factors[0], factors[1], norm.reshape(-1).astype(jnp.bfloat16)


def solution(mesh):
    return jax.shard_map(
        functools.partial(shards, mesh.shape["shard"], mesh.shape["tp"]),
        mesh=mesh,
        in_specs=(
            P("shard", "tp"),
            P("shard", "tp"),
            P("shard", "tp"),
            P("shard", "tp"),
            P("shard"),
            P(("shard", "tp")),
            P(("shard", "tp")),
        ),
        out_specs=(P(None, "tp"), P(None, "tp"), P("tp"), P("tp"), P()),
        check_vma=False,
    )
```

time: 329 us -> 186 us (0.57)
  waiting for transfers between devices: 207 us -> 0 us
  Pallas kernels: 0 us -> 182 us
  blocking collectives: 79.8 us -> 0 us
  local copies, waits for them, and re-layouts: 17.2 us -> 3.41 us
  between operations: 14.1 us -> 0.67 us
  other arithmetic: 10.8 us -> 0.06 us
    all_gather x2 -> x0, waiting for transfers between devices: 206 us -> none  [the longest x1 125 us: shards(): lax.all_gather(narrow_up, 'shard', axis=0, tiled=True)]
    pallas_call x0 -> x2, Pallas kernels: none -> 182 us  [the longest x1 176 us: shards(): pl.pallas_call(functools.partial(gather_kernel, n, parts, pieces), out_sh...]
    unnamed x1 -> x0, blocking collectives: 41 us -> none
    psum x1 -> x0, blocking collectives: 38.8 us -> none  [shards(): lax.psum((jnp.sum(fresh_gate * fresh_gate, axis=0), jnp.sum(fresh_up * fr...]
    unnamed x16 -> x4, local copies, waits for them, and re-layouts: 17.2 us -> 1.31 us
    convert_element_type x2 -> x1, other arithmetic: 5.36 us -> 0.06 us  [shards(): norm.reshape(-1).astype(jnp.bfloat16)]
    reduce_sum x1 -> x0, other arithmetic: 4.76 us -> none  [shards(): jnp.sum(fresh_up * fresh_up, axis=0)]
  transfers between devices with their start and end apart: 2 -> 0, of which waited for: 2 -> 0; matrix products, arithmetic and copies ran while one was open for 0% -> 0% of each run, Pallas kernels for 0% -> 0%
where the time goes in v1:
time: 186 us
  Pallas kernels  182 us (98%)
  local copies, waits for them, and re-layouts  3.41 us (2%)
    pallas_call x1, Pallas kernels, shards(): pl.pallas_call(functools.partial(gather_kernel, n, parts, pieces), out_sh...  176 us
    pallas_call x1, Pallas kernels, shards(): pl.pallas_call(functools.partial(write_kernel, n), out_shape=(jax.ShapeDt...  5.96 us

profile of v1, /device:TPU:0, one launch (start us, length us, event | category | flops | bytes accessed | tf_op | source)
XLA Modules:
  0.0 186.0 jit_solution(9235453061556622923)
XLA Ops:
  0.6 0.8 copy.12.mix
  1.4 0.0 copy-start
  1.5 0.6 copy-done
  2.1 0.0 copy-start.1
  2.1 0.7 copy-done.1
  2.8 175.9 %mix_gather.1 = (bf16[2,2048,2048]{2,1,0:T(8,128)(2,1)S(1)}, f32[2,2048]{1,0:T(2,128)S(1)}, f32[8,4,1,64]{3,2,1,0:T(1,128)S(1)}) custom-call(f32[256,2048]{1,0:T(8,128)} %one_gate.1, f32[256,2048]{1,0:T(8,128)} %other_gate.1, f32[256,2048]{1,0:T(8,128)} %one_up.1, f32[256,2048]{1,0:T(8,128)} %other_up.1, f32[256,1]{1,0:T(8,128)S(1)} %copy.12.mix, ...), custom_call_target="tpu_custom_call" | custom-call | tf_op jit(solution)/shard_map/mix_gather/pallas_call | solution.py:265
  178.7 6.0 %write_out.1 = (bf16[2048,2048]{1,0:T(8,128)(2,1)}, bf16[2048,2048]{1,0:T(8,128)(2,1)}) custom-call(bf16[2,2048,2048]{2,1,0:T(8,128)(2,1)S(1)} %get-tuple-element.10.held), custom_call_target="tpu_custom_call" | custom-call | tf_op jit(solution)/shard_map/write_out/pallas_call | solution.py:294
  184.6 0.1 convert_reduce_fusion
  184.7 0.7 convert_element_type.7
  185.4 0.6 fusion
Async XLA Ops:
  1.4 0.7 copy-start
  2.1 0.7 copy-start.1

commit v2 on v1

--- a/solution.py
+++ b/solution.py
@@ -13,8 +13,9 @@
 
 def gather_kernel(
     n, parts, pieces, one_gate, other_gate, one_up, other_up, mix, train, step,
-    held, factor, norm,
-    ones, others, sums, in_sem, sum_send, sum_recv, norm_send, norm_recv, send_sem, recv_sem,
+    held, factor_gate, factor_up, norm,
+    ones, others, sums, mix_row, shares, gains, in_sem, small_sem,
+    sum_send, sum_recv, norm_send, norm_recv, send_sem, recv_sem,
 ):
     me = lax.axis_index("shard")
     part = lax.axis_index("tp")
@@ -22,6 +23,22 @@
     place, side = me // 2, me % 2
     rows, cols = ones.shape[1:]
     tall = rows // half
+    lanes = shares.shape[1]
+
+    barrier = pltpu.get_barrier_semaphore()
+
+    @pl.loop(1, n)
+    def _(off):
+        pl.semaphore_signal(barrier, inc=1, device_id={"shard": lax.rem(me + off, n)}, device_id_type=MESH)
+
+    @pl.loop(1, parts)
+    def _(off):
+        pl.semaphore_signal(barrier, inc=1, device_id={"tp": lax.rem(part + off, parts)}, device_id_type=MESH)
+
+    read_mix = pltpu.make_async_copy(mix, mix_row, small_sem.at[0])
+    read_gains = [
+        pltpu.make_async_copy(source, gains.at[i], small_sem.at[1 + i]) for i, source in enumerate((train, step))
+    ]
 
     def reads(piece):
         a, at = piece // half, pl.ds(piece % half * tall, tall)
@@ -31,23 +48,53 @@
             pltpu.make_async_copy(second.at[at], others.at[a, at], in_sem.at[1, piece]),
         )
 
+    read_mix.start()
     for piece in range(pieces):
         for copy in reads(piece):
             copy.start()
-
-    barrier = pltpu.get_barrier_semaphore()
-
-    @pl.loop(1, n)
-    def _(off):
-        pl.semaphore_signal(barrier, inc=1, device_id={"shard": lax.rem(me + off, n)}, device_id_type=MESH)
-
-    @pl.loop(1, parts)
-    def _(off):
-        pl.semaphore_signal(barrier, inc=1, device_id={"tp": lax.rem(part + off, parts)}, device_id_type=MESH)
-
-    pl.semaphore_wait(barrier, n + parts - 2)
-
-    norm[me, part] = train[...] + step[...]
+    for copy in read_gains:
+        copy.start()
+    read_mix.wait()
+    shares[...] = jnp.transpose(jnp.broadcast_to(mix_row[...], (lanes, shares.shape[0])))
+
+    def mix_and_sum(a):
+        total = jnp.zeros((8, cols), jnp.float32)
+        for piece in range(a * half, (a + 1) * half):
+            for copy in reads(piece):
+                copy.wait()
+
+            def mixed(r, total):
+                at = pl.ds(pl.multiple_of(piece % half * tall + r * 8, 8), 8)
+                share = shares[at]
+                rest = 1.0 - share
+                share, rest = (jnp.concatenate([v] * (cols // lanes), axis=1) for v in (share, rest))
+                fresh = share * ones[a, at] + rest * others[a, at]
+                ones[a, at] = fresh
+                return total + fresh * fresh
+
+            total = lax.fori_loop(0, tall // 8, mixed, total, unroll=2)
+        sums[a, me] = jnp.sum(total, axis=0, keepdims=True)
+
+    def sum_copy(a, off):
+        return pltpu.make_async_remote_copy(
+            src_ref=sums.at[a, me], dst_ref=sums.at[a, me],
+            send_sem=sum_send.at[a, off], recv_sem=sum_recv.at[a, off],
+            device_id={"shard": lax.rem(me + off, n)}, device_id_type=MESH,
+        )
+
+    def exchange(a):
+        @pl.loop(1, n)
+        def _(off):
+            sum_copy(a, off).start()
+
+    def scales(a):
+        @pl.loop(1, n)
+        def _(off):
+            sum_copy(a, off).wait_recv()
+
+        factors = jnp.sqrt(lax.fori_loop(1, n, lambda i, t: t + sums[a, i], sums[a, 0]))
+        (factor_gate, factor_up)[a][...] = factors
+        return jnp.broadcast_to(1.0 / factors, (8, cols))
 
     def norm_row(off):
         return pltpu.make_async_remote_copy(
@@ -62,53 +109,6 @@
             send_sem=norm_send.at[parts + off], recv_sem=norm_recv.at[parts + off],
             device_id={"shard": lax.rem(me + off, n)}, device_id_type=MESH,
         )
-
-    @pl.loop(1, parts)
-    def _(off):
-        norm_row(off).start()
-
-    for a in range(2):
-        total = jnp.zeros((8, cols), jnp.float32)
-        for piece in range(a * half, (a + 1) * half):
-            for copy in reads(piece):
-                copy.wait()
-
-            def mixed(r, total):
-                at = pl.ds(pl.multiple_of(piece % half * tall + r * 8, 8), 8)
-                share = mix[at]
-                fresh = share * ones[a, at] + (1.0 - share) * others[a, at]
-                ones[a, at] = fresh
-                return total + fresh * fresh
-
-            total = lax.fori_loop(0, tall // 8, mixed, total)
-        sums[me, pl.ds(a, 1)] = jnp.sum(total, axis=0, keepdims=True)
-
-    def sum_copy(off):
-        return pltpu.make_async_remote_copy(
-            src_ref=sums.at[me], dst_ref=sums.at[me],
-            send_sem=sum_send.at[off], recv_sem=sum_recv.at[off],
-            device_id={"shard": lax.rem(me + off, n)}, device_id_type=MESH,
-        )
-
-    @pl.loop(1, n)
-    def _(off):
-        sum_copy(off).start()
-
-    @pl.loop(1, parts)
-    def _(off):
-        norm_row(off).wait()
-
-    @pl.loop(1, n)
-    def _(off):
-        norm_group(off).start()
-
-    @pl.loop(1, n)
-    def _(off):
-        sum_copy(off).wait_recv()
-
-    factors = jnp.sqrt(lax.fori_loop(1, n, lambda i, t: t + sums[i], sums[0]))
-    factor[...] = factors
-    scales = 1.0 / factors
 
     def piece_of(j, s, c):
         at = pl.multiple_of((2 * j + s) * rows + c % half * tall, 8)
@@ -140,28 +140,53 @@
         kept = kept & (c >= half)
         return ~(kept | ((place == 1) & (j == 0)) | ((place == last - 1) & (j == last)))
 
-    for c in range(pieces):
-        a, at = c // half, c % half * tall
-        scale = scales[a : a + 1]
-
-        def scaled(r, _):
-            here = pl.multiple_of(at + r * 8, 8)
-            there = pl.multiple_of(me * rows + at + r * 8, 8)
-            held[a, pl.ds(there, 8)] = (ones[a, pl.ds(here, 8)] * scale).astype(jnp.bfloat16)
-            return 0
-
-        lax.fori_loop(0, tall // 8, scaled, 0)
-
-        @pl.when(~last_place)
-        def _():
-            send(UP, place, side, c).start()
-
-        @pl.when(~first_place)
-        def _():
-            send(DOWN, place, side, c).start()
-
-        send(ACROSS, place, side, c).start()
-
+    def own(a):
+        scale = scales(a)
+        for c in range(a * half, (a + 1) * half):
+            at = c % half * tall
+
+            def scaled(r, _):
+                here = pl.multiple_of(at + r * 8, 8)
+                there = pl.multiple_of(me * rows + at + r * 8, 8)
+                held[a, pl.ds(there, 8)] = (ones[a, pl.ds(here, 8)] * scale).astype(jnp.bfloat16)
+                return 0
+
+            lax.fori_loop(0, tall // 8, scaled, 0, unroll=2)
+
+            @pl.when(~last_place)
+            def _():
+                send(UP, place, side, c).start()
+
+            @pl.when(~first_place)
+            def _():
+                send(DOWN, place, side, c).start()
+
+            send(ACROSS, place, side, c).start()
+
+    mix_and_sum(0)
+    pl.semaphore_wait(barrier, n + parts - 2)
+    exchange(0)
+    own(0)
+    for copy in read_gains:
+        copy.wait()
+    norm[me, part] = gains[0] + gains[1]
+
+    @pl.loop(1, parts)
+    def _(off):
+        norm_row(off).start()
+
+    mix_and_sum(1)
+    exchange(1)
+
+    @pl.loop(1, parts)
+    def _(off):
+        norm_row(off).wait()
+
+    @pl.loop(1, n)
+    def _(off):
+        norm_group(off).start()
+
+    own(1)
     extra = 3 * m
 
     def ends(b, c):
@@ -239,17 +264,20 @@
 
     @pl.loop(1, n)
     def _(off):
-        sum_copy(off).wait_send()
+        sum_copy(0, off).wait_send()
+        sum_copy(1, off).wait_send()
         norm_group(off).wait()
 
 
-def write_kernel(n, held, gate, up, sem):
+def write_kernel(n, held, factor_gate, factor_up, gate, up, out_gate, out_up, sem, small_sem):
     rows = held.shape[1] // n
     copies = [
         pltpu.make_async_copy(held.at[a, pl.ds(i * rows, rows)], out.at[pl.ds(i * rows, rows)], sem.at[a, i])
         for i in range(n)
         for a, out in enumerate((gate, up))
     ]
+    copies.append(pltpu.make_async_copy(factor_gate, out_gate, small_sem.at[0]))
+    copies.append(pltpu.make_async_copy(factor_up, out_up, small_sem.at[1]))
     for copy in copies:
         copy.start()
     for copy in copies:
@@ -259,48 +287,56 @@
 def shards(n, parts, one_gate, other_gate, one_up, other_up, mix_share, norm_train, norm_step):
     rows, cols = one_gate.shape
     few = norm_train.shape[0]
+    lanes = 128
+    padded = -(-rows // lanes) * lanes
     pieces = 2 * max(1, rows // 64)
     kinds = pltpu.SemaphoreType
     vmem, anywhere = pl.BlockSpec(memory_space=pltpu.VMEM), pl.BlockSpec(memory_space=pl.ANY)
-    held, factors, norm = pl.pallas_call(
+    held, factor_gate, factor_up, norm = pl.pallas_call(
         functools.partial(gather_kernel, n, parts, pieces),
         out_shape=(
             pltpu.VMEM((2, n * rows, cols), jnp.bfloat16),
-            jax.ShapeDtypeStruct((2, cols), jnp.float32),
-            jax.ShapeDtypeStruct((n, parts, 1, few), jnp.float32),
+            pltpu.VMEM((1, cols), jnp.float32),
+            pltpu.VMEM((1, cols), jnp.float32),
+            pltpu.VMEM((n, parts, 1, few), jnp.float32),
         ),
-        in_specs=[anywhere] * 4 + [vmem] * 3,
-        out_specs=(vmem, vmem, vmem),
+        in_specs=[pl.BlockSpec(memory_space=pltpu.HBM)] * 7,
+        out_specs=(vmem,) * 4,
         scratch_shapes=[
             pltpu.VMEM((2, rows, cols), jnp.float32),
             pltpu.VMEM((2, rows, cols), jnp.float32),
-            pltpu.VMEM((n, 2, cols), jnp.float32),
+            pltpu.VMEM((2, n, 1, cols), jnp.float32),
+            pltpu.VMEM((1, padded), jnp.float32),
+            pltpu.VMEM((padded, lanes), jnp.float32),
+            pltpu.VMEM((2, 1, few), jnp.float32),
             kinds.DMA((2, pieces)),
-            kinds.DMA((n,)),
-            kinds.DMA((n,)),
+            kinds.DMA((3,)),
+            kinds.DMA((2, n)),
+            kinds.DMA((2, n)),
             kinds.DMA((n + parts,)),
             kinds.DMA((n + parts,)),
             kinds.DMA((3 * (n // 2) + 1, pieces)),
             kinds.DMA((n, pieces)),
         ],
         compiler_params=pltpu.CompilerParams(
-            collective_id=0, has_side_effects=True, vmem_limit_bytes=36 * 2**20
+            collective_id=0, has_side_effects=True, vmem_limit_bytes=46 * 2**20
         ),
         name="mix_gather",
     )(
-        one_gate, other_gate, one_up, other_up, mix_share[:, None],
-        norm_train[None], norm_step[None],
+        one_gate, other_gate, one_up, other_up,
+        jnp.pad(mix_share, (0, padded - rows))[None], norm_train[None], norm_step[None],
     )
-    gate, up = pl.pallas_call(
+    gate, up, factor_gate, factor_up = pl.pallas_call(
         functools.partial(write_kernel, n),
-        out_shape=(jax.ShapeDtypeStruct((n * rows, cols), jnp.bfloat16),) * 2,
-        in_specs=[vmem],
-        out_specs=(anywhere, anywhere),
-        scratch_shapes=[kinds.DMA((2, n))],
-        compiler_params=pltpu.CompilerParams(vmem_limit_bytes=20 * 2**20),
+        out_shape=(jax.ShapeDtypeStruct((n * rows, cols), jnp.bfloat16),) * 2
+        + (jax.ShapeDtypeStruct((1, cols), jnp.float32),) * 2,
+        in_specs=[vmem] * 3,
+        out_specs=(anywhere,) * 4,
+        scratch_shapes=[kinds.DMA((2, n)), kinds.DMA((2,))],
+        compiler_params=pltpu.CompilerParams(vmem_limit_bytes=2**20),
         name="write_out",
-    )(held)
-    return gate, up, factors[0], factors[1], norm.reshape(-1).astype(jnp.bfloat16)
+    )(held, factor_gate, factor_up)
+    return gate, up, factor_gate[0], factor_up[0], norm.reshape(-1).astype(jnp.bfloat16)
 
 
 def solution(mesh):

time: 186 us -> 181 us (0.973)
  Pallas kernels: 182 us -> 179 us
  local copies, waits for them, and re-layouts: 3.41 us -> 0.68 us
    pallas_call x1, Pallas kernels: 176 us -> 173 us  [shards(): pl.pallas_call(functools.partial(gather_kernel, n, parts, pieces), out_sh...]
where the time goes in v2:
time: 181 us
  Pallas kernels  179 us (99%)
    pallas_call x1, Pallas kernels, shards(): pl.pallas_call(functools.partial(gather_kernel, n, parts, pieces), out_sh...  173 us
    pallas_call x1, Pallas kernels, shards(): pl.pallas_call(functools.partial(write_kernel, n), out_shape=(jax.ShapeDt...  5.99 us

profile of v2, /device:TPU:0, one launch (start us, length us, event | category | flops | bytes accessed | tf_op | source)
XLA Modules:
  0.0 180.7 jit_solution(18069503154790256064)
XLA Ops:
  0.6 173.3 %mix_gather.1 = (bf16[2,2048,2048]{2,1,0:T(8,128)(2,1)S(1)}, f32[1,2048]{1,0:T(1,128)S(1)}, f32[1,2048]{1,0:T(1,128)S(1)}, f32[8,4,1,64]{3,2,1,0:T(1,128)S(1)}) custom-call(f32[256,2048]{1,0:T(8,128)} %one_gate.1, f32[256,2048]{1,0:T(8,128)} %other_gate.1, f32[256,2048]{1,0:T(8,128)} %one_up.1, f32[256,2048]{1,0:T(8,128)} %other_up.1, f32[1,256]{1,0:T(1,128)} %bitcast.5, ...), custom_call_target="tpu_custom_call" | custom-call | tf_op jit(solution)/shard_map/mix_gather/pallas_call | solution.py:295
  174.0 6.0 %write_out.1 = (bf16[2048,2048]{1,0:T(8,128)(2,1)}, bf16[2048,2048]{1,0:T(8,128)(2,1)}, f32[1,2048]{1,0:T(1,128)}, f32[1,2048]{1,0:T(1,128)}) custom-call(bf16[2,2048,2048]{2,1,0:T(8,128)(2,1)S(1)} %get-tuple-element.13.held, f32[1,2048]{1,0:T(1,128)S(1)} %get-tuple-element.14.factor_gate, f32[1,2048]{1,0:T(1,128)S(1)} %get-tuple-element.15.factor_up), custom_call_target="tpu_custom_call" | custom-call | tf_op jit(solution)/shard_map/write_out/pallas_call | solution.py:329
  180.0 0.1 convert_reduce_fusion
  180.0 0.7 convert_element_type.7

commit v3 on v2

--- a/solution.py
+++ b/solution.py
@@ -49,11 +49,9 @@
         )
 
     read_mix.start()
-    for piece in range(pieces):
+    for piece in range(half):
         for copy in reads(piece):
             copy.start()
-    for copy in read_gains:
-        copy.start()
     read_mix.wait()
     shares[...] = jnp.transpose(jnp.broadcast_to(mix_row[...], (lanes, shares.shape[0])))
 
@@ -72,7 +70,7 @@
                 ones[a, at] = fresh
                 return total + fresh * fresh
 
-            total = lax.fori_loop(0, tall // 8, mixed, total, unroll=2)
+            total = lax.fori_loop(0, tall // 8, mixed, total, unroll=4)
         sums[a, me] = jnp.sum(total, axis=0, keepdims=True)
 
     def sum_copy(a, off):
@@ -151,7 +149,7 @@
                 held[a, pl.ds(there, 8)] = (ones[a, pl.ds(here, 8)] * scale).astype(jnp.bfloat16)
                 return 0
 
-            lax.fori_loop(0, tall // 8, scaled, 0, unroll=2)
+            lax.fori_loop(0, tall // 8, scaled, 0, unroll=4)
 
             @pl.when(~last_place)
             def _():
@@ -166,6 +164,11 @@
     mix_and_sum(0)
     pl.semaphore_wait(barrier, n + parts - 2)
     exchange(0)
+    for piece in range(half, pieces):
+        for copy in reads(piece):
+            copy.start()
+    for copy in read_gains:
+        copy.start()
     own(0)
     for copy in read_gains:
         copy.wait()
@@ -237,36 +240,47 @@
             def _():
                 send(DOWN, place, 1 - side, c, extra).start()
 
-    @pl.loop(0, m * pieces)
-    def _(slot):
-        j, c = slot // pieces, slot % pieces
-        passed_on = first_place | last_place | (((place == 1) | (place == last - 1)) & (c >= half))
-
-        @pl.when(~((j == place) & passed_on))
-        def _():
-            arrived(j, 1 - side, c)
-
-        @pl.when((j <= place) & ~last_place)
-        def _():
-            send(UP, j, side, c).wait_send()
-
-        @pl.when((j >= place) & ~first_place)
-        def _():
-            send(DOWN, j, side, c).wait_send()
-
-        @pl.when(crosses(j, c))
-        def _():
-            send(ACROSS, j, side, c).wait_send()
-
-        @pl.when((j == place) & passed_on)
-        def _():
-            send(UP, place, 1 - side, c, extra).wait_send()
+    passed_on = first_place | last_place
+    passed_half = (place == 1) | (place == last - 1)
+    inward = jnp.where(first_place, 1, last - 1)
 
     @pl.loop(1, n)
     def _(off):
         sum_copy(0, off).wait_send()
         sum_copy(1, off).wait_send()
         norm_group(off).wait()
+
+    @pl.loop(0, m * pieces)
+    def _(slot):
+        b, c = slot // pieces, slot % pieces
+        j = jnp.where(2 * place < last, b, last - b)
+        passed = (j == place) & (passed_on | (passed_half & (c >= half)))
+        late = passed_on & (j == inward) & (c >= half)
+
+        @pl.when((j <= place) & ~last_place)
+        def _():
+            send(UP, j, side, c).wait_send()
+
+        @pl.when((j >= place) & ~first_place)
+        def _():
+            send(DOWN, j, side, c).wait_send()
+
+        @pl.when(passed)
+        def _():
+            send(UP, place, 1 - side, c, extra).wait_send()
+
+        @pl.when(crosses(j, c))
+        def _():
+            send(ACROSS, j, side, c).wait_send()
+
+        @pl.when(~(passed | late))
+        def _():
+            arrived(j, 1 - side, c)
+
+    @pl.when(passed_on)
+    def _():
+        for c in range(half, pieces):
+            arrived(inward, 1 - side, c)
 
 
 def write_kernel(n, held, factor_gate, factor_up, gate, up, out_gate, out_up, sem, small_sem):

time: 181 us -> 180 us (level)
  no operation moved by 1% of the time
where the time goes in v3:
time: 180 us; the launch traced here: 179 us
  Pallas kernels  178 us (99%)
    pallas_call x1, Pallas kernels, shards(): pl.pallas_call(functools.partial(gather_kernel, n, parts, pieces), out_sh...  172 us
    pallas_call x1, Pallas kernels, shards(): pl.pallas_call(functools.partial(write_kernel, n), out_shape=(jax.ShapeDt...  5.99 us

profile of v3, /device:TPU:0, one launch (start us, length us, event | category | flops | bytes accessed | tf_op | source)
XLA Modules:
  0.0 179.4 jit_solution(7337711700212073556)
XLA Ops:
  0.6 172.0 %mix_gather.1 = (bf16[2,2048,2048]{2,1,0:T(8,128)(2,1)S(1)}, f32[1,2048]{1,0:T(1,128)S(1)}, f32[1,2048]{1,0:T(1,128)S(1)}, f32[8,4,1,64]{3,2,1,0:T(1,128)S(1)}) custom-call(f32[256,2048]{1,0:T(8,128)} %one_gate.1, f32[256,2048]{1,0:T(8,128)} %other_gate.1, f32[256,2048]{1,0:T(8,128)} %one_up.1, f32[256,2048]{1,0:T(8,128)} %other_up.1, f32[1,256]{1,0:T(1,128)} %bitcast.5, ...), custom_call_target="tpu_custom_call" | custom-call | tf_op jit(solution)/shard_map/mix_gather/pallas_call | solution.py:309
  172.7 6.0 %write_out.1 = (bf16[2048,2048]{1,0:T(8,128)(2,1)}, bf16[2048,2048]{1,0:T(8,128)(2,1)}, f32[1,2048]{1,0:T(1,128)}, f32[1,2048]{1,0:T(1,128)}) custom-call(bf16[2,2048,2048]{2,1,0:T(8,128)(2,1)S(1)} %get-tuple-element.13.held, f32[1,2048]{1,0:T(1,128)S(1)} %get-tuple-element.14.factor_gate, f32[1,2048]{1,0:T(1,128)S(1)} %get-tuple-element.15.factor_up), custom_call_target="tpu_custom_call" | custom-call | tf_op jit(solution)/shard_map/write_out/pallas_call | solution.py:343
  178.7 0.1 convert_reduce_fusion
  178.7 0.7 convert_element_type.7
